TPU v7x, 32 devices: a whole 2x2x4 slice. The times are simulated.
32 devices in a mesh: grp: 2 (over x), freq: 16 (over z, y, core).
Axes of the slice: x: 2, y: 2, z: 4, core: 2. Of those that a mesh axis runs over, the one named last changes fastest.
Arguments:
- kernel: bfloat16 [2, 256, 1024, 1024], P(None, ('grp', 'freq')), parts along dimension 1, may hold values from -0.125 to 0.125
- recorded: float32 [2, 256, 1024, 128], P(None, ('grp', 'freq')), parts along dimension 1, may hold values from -8 to 8
- onset_time: int32 [2048, 128], P(('grp', 'freq')), parts along dimension 0, may hold values from 32 to 256, as said below
Outputs:
- focusing: float32 [256, 2048, 128], P(None, ('grp', 'freq')), parts along dimension 1
There are 2 independent parts, one for each index of `grp`. A program takes and returns all parts, laid end to end along the dimension named above; each array names one. Nothing has to cross between parts.
Inputs may be any that keep to these rules, and one draw needn't show every extreme that they name: `onset_time`: onset sample of the window for each receiver and focal point.
All inputs are finite; a program needn't handle non-finite values.
Results may differ from a plain program's by a relative error of at most 0.012.
Values may be sent and summed in bfloat16 or wider, within the bound.
A program may use at most 192 MiB of HBM per device.

v0:
```python
import math
import jax
import jax.numpy as jnp
from jax import lax
from jax.sharding import PartitionSpec as P

NF = 128
ITERS = 2


def dft_tables():
    samples = jnp.arange(2 * NF, dtype=jnp.int32)
    bins = jnp.arange(NF, dtype=jnp.int32)
    phase = (bins[:, None] * samples[None, :] % (2 * NF)).astype(jnp.float32) * (math.pi / NF)
    factor = 1.0 / math.sqrt(NF)
    return (jnp.cos(phase) * factor, jnp.sin(phase) * factor)


def square_sum(values):
    return jnp.sum(values * values)


def joint_total(first, second, third):
    return lax.psum((first, second, third), "freq")


def body(kernel, recorded, onset_time):
    highest = lax.Precision.HIGHEST
    cosine_table, sin_tab = dft_tables()
    rec_local = onset_time.shape[0]
    focal_count = onset_time.shape[1]
    samples = lax.broadcasted_iota(jnp.int32, (2 * NF, rec_local, focal_count), 0)
    keep_mask = (samples < onset_time[None]).astype(jnp.float32)
    kernel_real = kernel[0]
    kernel_imaginary = kernel[1]

    def invert(block_in):
        columns = block_in.shape[3]
        widened = block_in.astype(jnp.float32)
        timed = jnp.dot(cosine_table.T, widened[0].reshape(NF, -1), precision=highest) - jnp.dot(
            sin_tab.T, widened[1].reshape(NF, -1), precision=highest
        )
        return timed.reshape(2 * NF, block_in.shape[2], columns)

    def apply_adjoint(resid):
        rounded = resid.astype(jnp.bfloat16)
        update_real = rounded[0]
        update_imaginary = rounded[1]
        z_real = jnp.einsum(
            "hvi,hvg->hig", kernel_real, update_real, preferred_element_type=jnp.float32
        ) + jnp.einsum(
            "hvi,hvg->hig", kernel_imaginary, update_imaginary, preferred_element_type=jnp.float32
        )
        z_imag = jnp.einsum(
            "hvi,hvg->hig", kernel_real, update_imaginary, preferred_element_type=jnp.float32
        ) - jnp.einsum(
            "hvi,hvg->hig", kernel_imaginary, update_real, preferred_element_type=jnp.float32
        )
        image = jnp.stack([z_real, z_imag]).astype(jnp.bfloat16)
        timed = invert(lax.all_to_all(image, "freq", split_axis=2, concat_axis=1, tiled=True))
        return timed * keep_mask

    model_raw = apply_adjoint(recorded)
    totals = joint_total(square_sum(recorded), square_sum(model_raw), jnp.float32(0.0))
    beta_now = jnp.sqrt(totals[0])
    data_vec = recorded / beta_now
    alpha_now = jnp.sqrt(totals[1]) / beta_now
    model_vec = model_raw / (alpha_now * beta_now)
    search = model_vec
    estimate = jnp.zeros_like(model_vec)
    phibar_now = beta_now
    rhobar_now = alpha_now
    for iteration in range(ITERS):
        flat_part = (model_vec * keep_mask).reshape(2 * NF, -1)
        spec_real = jnp.dot(cosine_table, flat_part, precision=highest)
        spec_imag = -jnp.dot(sin_tab, flat_part, precision=highest)
        spectrum = (
            jnp.stack([spec_real, spec_imag])
            .reshape(2, NF, rec_local, focal_count)
            .astype(jnp.bfloat16)
        )
        multiply_block_in = lax.all_to_all(
            spectrum, "freq", split_axis=1, concat_axis=2, tiled=True
        )
        solution_real = multiply_block_in[0]
        solution_imaginary = multiply_block_in[1]
        y_real = jnp.einsum(
            "ptx,pxi->pti", kernel_real, solution_real, preferred_element_type=jnp.float32
        ) - jnp.einsum(
            "ptx,pxi->pti", kernel_imaginary, solution_imaginary, preferred_element_type=jnp.float32
        )
        y_imag = jnp.einsum(
            "ptx,pxi->pti", kernel_real, solution_imaginary, preferred_element_type=jnp.float32
        ) + jnp.einsum(
            "ptx,pxi->pti", kernel_imaginary, solution_real, preferred_element_type=jnp.float32
        )
        data_raw = jnp.stack([y_real, y_imag]) - alpha_now * data_vec
        image_raw = apply_adjoint(data_raw)
        totals = joint_total(
            square_sum(data_raw), square_sum(image_raw), jnp.sum(image_raw * model_vec)
        )
        beta_now = jnp.sqrt(totals[0])
        data_vec = data_raw / beta_now
        alpha_now = jnp.sqrt(
            totals[1] / (beta_now * beta_now) - 2.0 * totals[2] + beta_now * beta_now
        )
        model_vec = (image_raw / beta_now - beta_now * model_vec) / alpha_now
        rho_now = jnp.sqrt(rhobar_now * rhobar_now + beta_now * beta_now)
        cosine = rhobar_now / rho_now
        sine_part = beta_now / rho_now
        theta_now = sine_part * alpha_now
        rhobar_now = -cosine * alpha_now
        phi_now = cosine * phibar_now
        phibar_now = sine_part * phibar_now
        estimate = estimate + phi_now / rho_now * search
        search = model_vec - theta_now / rho_now * search
    return estimate


def solution(mesh):
    placed = (
        P(None, ("grp", "freq"), None, None),
        P(None, ("grp", "freq"), None, None),
        P(("grp", "freq"), None),
    )
    return jax.shard_map(
        body, mesh=mesh, in_specs=placed, out_specs=P(None, ("grp", "freq"), None), check_vma=False
    )
```

profile of v0, /device:TPU:0, one launch (start us, length us, event | category | flops | bytes accessed | tf_op | source)
XLA Modules:
  0.0 832.4 jit_solution(1631037788863570241)
XLA Ops:
  8.5 10.8 %fusion.14 = f32[8,1024,128]{2,1,0:T(8,128)} fusion(bf16[2,8,1024,1024]{3,2,1,0:T(8,128)(2,1)} %param.3, bf16[2,8,1024,128]{3,2,1,0:T(8,128)(2,1)S(1)} %get-tuple-element.15), kind=kOutput, calls=%fused_computation.14 | convolution fusion | flops 2147483648 | bytes 23068672 | tf_op jit(solution)/shard_map/hvi,hvg->hig/dot_general | solution.py:51
  19.4 10.7 %fusion.12 = f32[8,1024,128]{2,1,0:T(8,128)} fusion(bf16[2,8,1024,1024]{3,2,1,0:T(8,128)(2,1)} %param.3, bf16[2,8,1024,128]{3,2,1,0:T(8,128)(2,1)S(1)} %get-tuple-element.15), kind=kOutput, calls=%fused_computation.12 | convolution fusion | flops 2147483648 | bytes 23068672 | tf_op jit(solution)/shard_map/hvi,hvg->hig/dot_general | solution.py:56
  39.7 10.4 %fusion.68 = bf16[1,8,1024,128]{3,2,1,0:T(8,128)(2,1)S(1)} fusion(f32[8,1024,128]{2,1,0:T(8,128)} %fusion.12, bf16[2,8,1024,128]{3,2,1,0:T(8,128)(2,1)S(1)} %get-tuple-element.15, bf16[2,8,1024,1024]{3,2,1,0:T(8,128)(2,1)} %param.3), kind=kOutput, calls=%fused_computation.98 | convolution fusion | flops 2149580800 | bytes 25165824 | tf_op jit(solution)/shard_map/hvi,hvg->hig/dot_general | solution.py:54
  53.2 99.3 %all_to_all.60 = bf16[2,8,1024,128]{3,1,0,2:T(8,128)(2,1)S(1)} all-to-all(bf16[2,8,1024,128]{3,1,0,2:T(8,128)(2,1)S(1)} %copy.81), channel_id=1, replica_groups=mesh['grp'=2,'freq'=16] {'freq'}, dimensions={2} | all-to-all | bytes 8388608 | tf_op jit(solution)/shard_map/all_to_all | solution.py:60
  159.0 12.1 %multiply_reduce_fusion.4 = (f32[]{:T(128)}, f32[256,8192]{1,0:T(8,128)}) fusion(s32[8192]{0:T(1024)S(1)} %bitcast.250, f32[256,8192]{1,0:T(8,128)S(1)} %fusion.78, bf16[16,8,64,128]{3,2,1,0:T(8,128)(2,1)S(1)} %get-tuple-element.22), kind=kOutput, calls=%fused_computation.58 | convolution fusion | flops 3232202752 | bytes 18907140 | tf_op jit(solution)/shard_map/dot_general | solution.py:40
  171.1 34.1 %all-reduce.1 = (f32[]{:T(128)}, f32[]{:T(128)}) all-reduce(f32[]{:T(128)} %get-tuple-element.24, f32[]{:T(128)} %get-tuple-element.14), channel_id=1, replica_groups=mesh['grp'=2,'freq'=16] {'freq'}, use_global_device_ids=true, to_apply=%region_1.2 | all-reduce | flops 2 | bytes 16 | tf_op jit(solution)/shard_map/psum | solution.py:24
  206.5 10.7 %fusion.89 = bf16[16,8,64,128]{3,1,2,0:T(8,128)(2,1)S(1)} fusion(s32[8192]{0:T(1024)S(1)} %bitcast.251, f32[256,8192]{1,0:T(8,128)} %get-tuple-element.25, f32[]{:T(128)S(6)} %mul.210), kind=kOutput, calls=%fused_computation.123 | convolution fusion | flops 3231154176 | bytes 10518532 | tf_op jit(solution)/shard_map/dot_general | solution.py:75
  242.5 68.8 %all-to-all-done.1 = bf16[2,128,64,128]{3,2,0,1:T(8,128)(2,1)} async-done(((bf16[2,128,64,128]{3,2,0,1:T(8,128)(2,1)}), bf16[2,128,64,128]{3,2,0,1:T(8,128)(2,1)}, u32[]{:S(2)}, u32[]{:S(2)}) %all-to-all-start.1) | async-done | bytes 4194336 | tf_op jit(solution)/shard_map/all_to_all | solution.py:82
  316.9 14.0 %fusion.10 = f32[8,128,1024]{2,1,0:T(8,128)} fusion(bf16[8,1024,128]{2,1,0:T(8,128)(2,1)} %bitcast.241, bf16[2,8,1024,1024]{3,2,1,0:T(8,128)(2,1)} %param.3), kind=kOutput, calls=%fused_computation.10 | convolution fusion | flops 2147483648 | bytes 23068672 | tf_op jit(solution)/shard_map/ptx,pxi->pti/dot_general | solution.py:89
  332.5 14.0 %fusion.8 = f32[8,128,1024]{2,1,0:T(8,128)} fusion(bf16[8,1024,128]{2,1,0:T(8,128)(2,1)} %bitcast.246, bf16[2,8,1024,1024]{3,2,1,0:T(8,128)(2,1)} %param.3), kind=kOutput, calls=%fused_computation.8 | convolution fusion | flops 2147483648 | bytes 23068672 | tf_op jit(solution)/shard_map/ptx,pxi->pti/dot_general | solution.py:94
  346.5 10.8 %subtract_bitcast_fusion.1 = f32[1,8,1024,128]{2,3,1,0:T(8,128)S(1)} fusion(f32[8,128,1024]{2,1,0:T(8,128)} %fusion.10, bf16[8,1024,128]{2,1,0:T(8,128)(2,1)} %bitcast.247, bf16[2,8,1024,1024]{3,2,1,0:T(8,128)(2,1)} %param.3), kind=kOutput, calls=%fused_computation.74 | convolution fusion | flops 2148532224 | bytes 27262976 | tf_op jit(solution)/shard_map/ptx,pxi->pti/dot_general | solution.py:87
  357.3 11.2 %add_bitcast_fusion.1 = f32[1,8,1024,128]{2,3,1,0:T(8,128)} fusion(f32[8,128,1024]{2,1,0:T(8,128)} %fusion.8, bf16[8,1024,128]{2,1,0:T(8,128)(2,1)S(1)} %bitcast.242, bf16[2,8,1024,1024]{3,2,1,0:T(8,128)(2,1)} %param.3), kind=kOutput, calls=%fused_computation.73 | convolution fusion | flops 2148532224 | bytes 27262976 | tf_op jit(solution)/shard_map/ptx,pxi->pti/dot_general | solution.py:92
  378.8 10.1 %fusion.6 = f32[8,128,1024]{2,1,0:T(8,128)} fusion(bf16[2,8,1024,1024]{3,2,1,0:T(8,128)(2,1)} %param.3, bf16[2,8,1024,128]{2,3,1,0:T(8,128)(2,1)S(1)} %convert_element_type.32), kind=kOutput, calls=%fused_computation.6 | convolution fusion | flops 2147483648 | bytes 23068672 | tf_op jit(solution)/shard_map/hvi,hvg->hig/dot_general | solution.py:51
  388.9 10.1 %fusion.4 = f32[8,128,1024]{2,1,0:T(8,128)} fusion(bf16[2,8,1024,1024]{3,2,1,0:T(8,128)(2,1)} %param.3, bf16[2,8,1024,128]{2,3,1,0:T(8,128)(2,1)S(1)} %convert_element_type.32), kind=kOutput, calls=%fused_computation.4 | convolution fusion | flops 2147483648 | bytes 23068672 | tf_op jit(solution)/shard_map/hvi,hvg->hig/dot_general | solution.py:56
  408.5 10.8 %fusion.70 = bf16[1,8,1024,128]{2,3,1,0:T(8,128)(2,1)} fusion(f32[8,128,1024]{2,1,0:T(8,128)} %fusion.4, bf16[2,8,1024,1024]{3,2,1,0:T(8,128)(2,1)} %param.3, bf16[2,8,1024,128]{2,3,1,0:T(8,128)(2,1)S(1)} %convert_element_type.32), kind=kOutput, calls=%fused_computation.100 | convolution fusion | flops 2149580800 | bytes 25165824 | tf_op jit(solution)/shard_map/hvi,hvg->hig/dot_general | solution.py:54
  430.2 112.1 %all_to_all.61 = bf16[2,8,1024,128]{3,1,0,2:T(8,128)(2,1)S(1)} all-to-all(bf16[2,8,1024,128]{3,1,0,2:T(8,128)(2,1)} %copy.101), channel_id=1, replica_groups=mesh['grp'=2,'freq'=16] {'freq'}, dimensions={2} | all-to-all | bytes 8388608 | tf_op jit(solution)/shard_map/all_to_all | solution.py:60
  549.1 11.3 %multiply_reduce_fusion = (f32[]{:T(128)}, f32[]{:T(128)}, f32[256,8192]{1,0:T(8,128)}) fusion(s32[8192]{0:T(1024)S(1)} %bitcast.253, f32[]{:T(128)S(6)} %mul.210, f32[256,8192]{1,0:T(8,128)S(1)} %bitcast.229, f32[256,8192]{1,0:T(8,128)S(1)} %fusion.73, bf16[16,8,64,128]{3,2,1,0:T(8,128)(2,1)S(1)} %bitcast.245), kind=kOutput, calls=%fused_computation.53 | convolution fusion | flops 3240591360 | bytes 27295756 | tf_op jit(solution)/shard_map/dot_general | solution.py:40
  560.4 34.2 %all-reduce = (f32[]{:T(128)}, f32[]{:T(128)}, f32[]{:T(128)}) all-reduce(f32[]{:T(128)} %get-tuple-element.12, f32[]{:T(128)} %get-tuple-element.6, f32[]{:T(128)} %get-tuple-element.5), channel_id=1, replica_groups=mesh['grp'=2,'freq'=16] {'freq'}, use_global_device_ids=true, to_apply=%region_5.6 | all-reduce | flops 3 | bytes 24 | tf_op jit(solution)/shard_map/psum | solution.py:24
  632.4 68.8 %all-to-all-done.3 = bf16[2,128,64,128]{3,2,0,1:T(8,128)(2,1)} async-done(((bf16[2,128,64,128]{3,2,0,1:T(8,128)(2,1)}), bf16[2,128,64,128]{3,2,0,1:T(8,128)(2,1)}, u32[]{:S(2)}, u32[]{:S(2)}) %all-to-all-start.3) | async-done | bytes 4194336 | tf_op jit(solution)/shard_map/all_to_all | solution.py:82
  706.8 14.0 %fusion.2 = f32[8,128,1024]{2,1,0:T(8,128)} fusion(bf16[8,1024,128]{2,1,0:T(8,128)(2,1)} %bitcast.243, bf16[2,8,1024,1024]{3,2,1,0:T(8,128)(2,1)} %param.3), kind=kOutput, calls=%fused_computation.2 | convolution fusion | flops 2147483648 | bytes 23068672 | tf_op jit(solution)/shard_map/ptx,pxi->pti/dot_general | solution.py:89
  722.4 14.3 %fusion = f32[8,128,1024]{2,1,0:T(8,128)} fusion(bf16[8,1024,128]{2,1,0:T(8,128)(2,1)} %bitcast.248, bf16[2,8,1024,1024]{3,2,1,0:T(8,128)(2,1)} %param.3), kind=kOutput, calls=%fused_computation | convolution fusion | flops 2147483648 | bytes 23068672 | tf_op jit(solution)/shard_map/ptx,pxi->pti/dot_general | solution.py:94
  736.8 10.7 %subtract_bitcast_fusion = f32[1,8,1024,128]{2,3,1,0:T(8,128)S(1)} fusion(f32[8,128,1024]{2,1,0:T(8,128)} %fusion.2, bf16[8,1024,128]{2,1,0:T(8,128)(2,1)} %bitcast.249, bf16[2,8,1024,1024]{3,2,1,0:T(8,128)(2,1)} %param.3), kind=kOutput, calls=%fused_computation.70 | convolution fusion | flops 2148532224 | bytes 27262976 | tf_op jit(solution)/shard_map/ptx,pxi->pti/dot_general | solution.py:87
  747.4 11.2 %add_bitcast_fusion = f32[1,8,1024,128]{2,3,1,0:T(8,128)} fusion(f32[8,128,1024]{2,1,0:T(8,128)} %fusion, bf16[8,1024,128]{2,1,0:T(8,128)(2,1)S(1)} %bitcast.244, bf16[2,8,1024,1024]{3,2,1,0:T(8,128)(2,1)} %param.3), kind=kOutput, calls=%fused_computation.69 | convolution fusion | flops 2148532224 | bytes 27262976 | tf_op jit(solution)/shard_map/ptx,pxi->pti/dot_general | solution.py:92
  773.2 48.3 %psum.47 = f32[]{:T(128)} all-reduce(f32[]{:T(128)} %fusion.40), channel_id=1, replica_groups=mesh['grp'=2,'freq'=16] {'freq'}, use_global_device_ids=true, to_apply=%region_11.12 | all-reduce | flops 1 | bytes 8 | tf_op jit(solution)/shard_map/psum | solution.py:24
  (60 shorter events, 164.4 us)
Async XLA Ops:
  154.5 4.4 copy-start.4
  206.5 10.7 %copy-start = (f32[256,8192]{1,0:T(8,128)S(1)}, f32[256,8192]{1,0:T(8,128)}, u32[]{:S(2)}) copy-start(f32[256,8192]{1,0:T(8,128)} %get-tuple-element.25) | copy-start | bytes 25165828
  229.2 82.0 %all-to-all-start.1 = ((bf16[2,128,64,128]{3,2,0,1:T(8,128)(2,1)}), bf16[2,128,64,128]{3,2,0,1:T(8,128)(2,1)}, u32[]{:S(2)}, u32[]{:S(2)}) async-start(bf16[2,128,64,128]{3,2,0,1:T(8,128)(2,1)} %pad_maximum_fusion.1), calls=%async_computation.1 | async-start | bytes 8388608 | tf_op jit(solution)/shard_map/all_to_all | solution.py:82
  346.5 10.8 %copy-start.2 = (bf16[1,8,16,64,128]{4,3,2,1,0:T(8,128)(2,1)S(1)}, bf16[1,8,16,64,128]{4,3,2,1,0:T(8,128)(2,1)}, u32[]{:S(2)}) copy-start(bf16[1,8,16,64,128]{4,3,2,1,0:T(8,128)(2,1)} %copy.89) | copy-start | bytes 6291460
  374.9 3.2 copy-start.1
  543.4 5.7 slice-start
  544.6 4.5 slice-start.1
  619.1 82.0 %all-to-all-start.3 = ((bf16[2,128,64,128]{3,2,0,1:T(8,128)(2,1)}), bf16[2,128,64,128]{3,2,0,1:T(8,128)(2,1)}, u32[]{:S(2)}, u32[]{:S(2)}) async-start(bf16[2,128,64,128]{3,2,0,1:T(8,128)(2,1)} %pad_maximum_fusion.3), calls=%async_computation.3 | async-start | bytes 8388608 | tf_op jit(solution)/shard_map/all_to_all | solution.py:82
  736.7 10.7 %copy-start.3 = (bf16[1,8,16,64,128]{4,3,2,1,0:T(8,128)(2,1)S(1)}, bf16[1,8,16,64,128]{4,3,2,1,0:T(8,128)(2,1)}, u32[]{:S(2)}) copy-start(bf16[1,8,16,64,128]{4,3,2,1,0:T(8,128)(2,1)} %copy.111) | copy-start | bytes 6291460
where the time goes:
time: 836 us; the launch traced here: 832 us
  blocking collectives  328 us (39%)
  matrix products  244 us (29%)
  waiting for transfers between devices  138 us (17%)
  local copies, waits for them, and re-layouts  60.7 us (7%)
  other arithmetic  47.7 us (6%)
  starting transfers between devices  9.31 us (1%)
    all_to_all x2, blocking collectives, apply_adjoint(): lax.all_to_all(image, 'freq', split_axis=2, concat_axis=1, tiled=True)  211 us
    all_to_all x2, waiting for transfers between devices, body(): lax.all_to_all(spectrum, 'freq', split_axis=1, concat_axis=2, tiled=True)  138 us
    psum x3, blocking collectives, joint_total(): return lax.psum((first, second, third), 'freq')  117 us
    unnamed x22, local copies, waits for them, and re-layouts  31.8 us
    dot_general x2, matrix products, body(): jnp.einsum('ptx,pxi->pti', kernel_imaginary, solution_real, preferred_ele...  28.3 us
    dot_general x2, matrix products, body(): jnp.einsum('ptx,pxi->pti', kernel_imaginary, solution_imaginary, preferre...  28 us
    dot_general x2, matrix products, invert(): jnp.dot(sin_tab.T, widened[1].reshape(NF, -1), precision=highest)  23.4 us
    dot_general x2, matrix products, body(): jnp.einsum('ptx,pxi->pti', kernel_real, solution_imaginary, preferred_ele...  22.4 us
  transfers between devices with their start and end apart: 2, of which 2 were waited for; matrix products, arithmetic and copies ran while one was open for 2% of the time, Pallas kernels for 0%

commit v1 on v0

--- a/solution.py
+++ b/solution.py
@@ -6,6 +6,13 @@
 
 NF = 128
 ITERS = 2
+
+
+def exchange_blocks(shard, axis, split, join):
+    size = lax.axis_size(axis)
+    shards = jnp.stack(jnp.split(shard, size, axis=split), axis=0)
+    shards = lax.all_to_all(shards, axis, split_axis=0, concat_axis=0)
+    return jnp.concatenate(shards, axis=join)
 
 
 def dft_tables():
@@ -57,7 +64,7 @@
             "hvi,hvg->hig", kernel_imaginary, update_real, preferred_element_type=jnp.float32
         )
         image = jnp.stack([z_real, z_imag]).astype(jnp.bfloat16)
-        timed = invert(lax.all_to_all(image, "freq", split_axis=2, concat_axis=1, tiled=True))
+        timed = invert(exchange_blocks(image, "freq", 2, 1))
         return timed * keep_mask
 
     model_raw = apply_adjoint(recorded)

time: 836 us -> 845 us (1.011)
  other arithmetic: 47.7 us -> 60.1 us
    unnamed x1 -> x31, other arithmetic: 0.01 us -> 15.6 us
    unnamed x22 -> x27, local copies, waits for them, and re-layouts: 31.8 us -> 33.5 us
where the time goes in v1:
time: 845 us; the launch traced here: 842 us
  blocking collectives  328 us (39%)
  matrix products  244 us (29%)
  waiting for transfers between devices  137 us (16%)
  other arithmetic  60.1 us (7%)
  local copies, waits for them, and re-layouts  57.8 us (7%)
  starting transfers between devices  9.5 us (1%)
    all_to_all x2, blocking collectives, exchange_blocks(): shards = lax.all_to_all(shards, axis, split_axis=0, concat_axis=0)  211 us
    all_to_all x2, waiting for transfers between devices, body(): lax.all_to_all(spectrum, 'freq', split_axis=1, concat_axis=2, tiled=True)  137 us
    psum x3, blocking collectives, joint_total(): return lax.psum((first, second, third), 'freq')  117 us
    unnamed x27, local copies, waits for them, and re-layouts  33.5 us
    dot_general x2, matrix products, body(): jnp.einsum('ptx,pxi->pti', kernel_imaginary, solution_real, preferred_ele...  28.3 us
    dot_general x2, matrix products, body(): jnp.einsum('ptx,pxi->pti', kernel_imaginary, solution_imaginary, preferre...  28.1 us
    dot_general x2, matrix products, invert(): jnp.dot(sin_tab.T, widened[1].reshape(NF, -1), precision=highest)  23.4 us
    dot_general x2, matrix products, apply_adjoint(): jnp.einsum('hvi,hvg->hig', kernel_imaginary, update_imaginary, preferred_...  22.4 us
  transfers between devices with their start and end apart: 2, of which 2 were waited for; matrix products, arithmetic and copies ran while one was open for 2% of the time, Pallas kernels for 0%

profile of v1, /device:TPU:0, one launch (start us, length us, event | category | flops | bytes accessed | tf_op | source)
XLA Modules:
  0.0 841.9 jit_solution(9579811482465128814)
XLA Ops:
  8.5 10.8 %fusion.14 = f32[8,1024,128]{2,1,0:T(8,128)} fusion(bf16[2,8,1024,1024]{3,2,1,0:T(8,128)(2,1)} %param.3, bf16[2,8,1024,128]{3,2,1,0:T(8,128)(2,1)S(1)} %get-tuple-element.15), kind=kOutput, calls=%fused_computation.14 | convolution fusion | flops 2147483648 | bytes 23068672 | tf_op jit(solution)/shard_map/hvi,hvg->hig/dot_general | solution.py:58
  19.3 10.7 %fusion.12 = f32[8,1024,128]{2,1,0:T(8,128)} fusion(bf16[2,8,1024,1024]{3,2,1,0:T(8,128)(2,1)} %param.3, bf16[2,8,1024,128]{3,2,1,0:T(8,128)(2,1)S(1)} %get-tuple-element.15), kind=kOutput, calls=%fused_computation.12 | convolution fusion | flops 2147483648 | bytes 23068672 | tf_op jit(solution)/shard_map/hvi,hvg->hig/dot_general | solution.py:63
  39.7 10.2 %fusion.68 = bf16[1,8,1024,128]{3,2,1,0:T(8,128)(2,1)S(1)} fusion(f32[8,1024,128]{2,1,0:T(8,128)} %fusion.12, bf16[2,8,1024,128]{3,2,1,0:T(8,128)(2,1)S(1)} %get-tuple-element.15, bf16[2,8,1024,1024]{3,2,1,0:T(8,128)(2,1)} %param.3), kind=kOutput, calls=%fused_computation.155 | convolution fusion | flops 2149580800 | bytes 25165824 | tf_op jit(solution)/shard_map/hvi,hvg->hig/dot_general | solution.py:61
  50.6 99.3 %all_to_all.40 = bf16[16,2,8,64,128]{4,3,2,1,0:T(8,128)(2,1)S(1)} all-to-all(bf16[16,2,8,64,128]{4,3,2,1,0:T(8,128)(2,1)S(1)} %fusion.138), channel_id=1, replica_groups=mesh['grp'=2,'freq'=16] {'freq'}, dimensions={0} | all-to-all | bytes 8388608 | tf_op jit(solution)/shard_map/all_to_all | solution.py:14
  155.9 12.1 %multiply_reduce_fusion.4 = (f32[]{:T(128)}, f32[256,8192]{1,0:T(8,128)}) fusion(s32[8192]{0:T(1024)S(1)} %bitcast.312, f32[256,8192]{1,0:T(8,128)S(1)} %fusion.78, bf16[16,8,64,128]{3,2,1,0:T(8,128)(2,1)S(1)} %get-tuple-element.22), kind=kOutput, calls=%fused_computation.118 | convolution fusion | flops 3232202752 | bytes 18907140 | tf_op jit(solution)/shard_map/dot_general | solution.py:47
  168.0 34.1 %all-reduce.1 = (f32[]{:T(128)}, f32[]{:T(128)}) all-reduce(f32[]{:T(128)} %get-tuple-element.24, f32[]{:T(128)} %get-tuple-element.14), channel_id=1, replica_groups=mesh['grp'=2,'freq'=16] {'freq'}, use_global_device_ids=true, to_apply=%region_1.2 | all-reduce | flops 2 | bytes 16 | tf_op jit(solution)/shard_map/psum | solution.py:31
  203.4 10.7 %fusion.89 = bf16[16,8,64,128]{3,1,2,0:T(8,128)(2,1)S(1)} fusion(s32[8192]{0:T(1024)S(1)} %bitcast.313, f32[256,8192]{1,0:T(8,128)} %get-tuple-element.25, f32[]{:T(128)S(6)} %mul.210), kind=kOutput, calls=%fused_computation.180 | convolution fusion | flops 3231154176 | bytes 10518532 | tf_op jit(solution)/shard_map/dot_general | solution.py:82
  239.1 68.8 %all-to-all-done.1 = bf16[2,128,64,128]{3,2,0,1:T(8,128)(2,1)} async-done(((bf16[2,128,64,128]{3,2,0,1:T(8,128)(2,1)}), bf16[2,128,64,128]{3,2,0,1:T(8,128)(2,1)}, u32[]{:S(2)}, u32[]{:S(2)}) %all-to-all-start.1) | async-done | bytes 4194336 | tf_op jit(solution)/shard_map/all_to_all | solution.py:89
  313.6 14.0 %fusion.10 = f32[8,128,1024]{2,1,0:T(8,128)} fusion(bf16[8,1024,128]{2,1,0:T(8,128)(2,1)} %bitcast.304, bf16[2,8,1024,1024]{3,2,1,0:T(8,128)(2,1)} %param.3), kind=kOutput, calls=%fused_computation.10 | convolution fusion | flops 2147483648 | bytes 23068672 | tf_op jit(solution)/shard_map/ptx,pxi->pti/dot_general | solution.py:96
  329.1 14.0 %fusion.8 = f32[8,128,1024]{2,1,0:T(8,128)} fusion(bf16[8,1024,128]{2,1,0:T(8,128)(2,1)} %bitcast.308, bf16[2,8,1024,1024]{3,2,1,0:T(8,128)(2,1)} %param.3), kind=kOutput, calls=%fused_computation.8 | convolution fusion | flops 2147483648 | bytes 23068672 | tf_op jit(solution)/shard_map/ptx,pxi->pti/dot_general | solution.py:101
  343.2 11.1 %subtract_bitcast_fusion.1 = f32[1,8,1024,128]{2,3,1,0:T(8,128)S(1)} fusion(f32[8,128,1024]{2,1,0:T(8,128)} %fusion.10, bf16[8,1024,128]{2,1,0:T(8,128)(2,1)} %bitcast.309, bf16[2,8,1024,1024]{3,2,1,0:T(8,128)(2,1)} %param.3), kind=kOutput, calls=%fused_computation.131 | convolution fusion | flops 2148532224 | bytes 27262976 | tf_op jit(solution)/shard_map/ptx,pxi->pti/dot_general | solution.py:94
  354.3 11.2 %add_bitcast_fusion.1 = f32[1,8,1024,128]{2,3,1,0:T(8,128)} fusion(f32[8,128,1024]{2,1,0:T(8,128)} %fusion.8, bf16[8,1024,128]{2,1,0:T(8,128)(2,1)S(1)} %bitcast.305, bf16[2,8,1024,1024]{3,2,1,0:T(8,128)(2,1)} %param.3), kind=kOutput, calls=%fused_computation.130 | convolution fusion | flops 2148532224 | bytes 27262976 | tf_op jit(solution)/shard_map/ptx,pxi->pti/dot_general | solution.py:99
  375.8 11.6 %fusion.6 = f32[8,128,1024]{2,1,0:T(8,128)} fusion(bf16[2,8,1024,1024]{3,2,1,0:T(8,128)(2,1)} %param.3, bf16[2,8,1024,128]{2,3,1,0:T(8,128)(2,1)S(1)} %convert_element_type.32), kind=kOutput, calls=%fused_computation.6 | convolution fusion | flops 2147483648 | bytes 23068672 | tf_op jit(solution)/shard_map/hvi,hvg->hig/dot_general | solution.py:58
  387.4 10.1 %fusion.4 = f32[8,128,1024]{2,1,0:T(8,128)} fusion(bf16[2,8,1024,1024]{3,2,1,0:T(8,128)(2,1)} %param.3, bf16[2,8,1024,128]{2,3,1,0:T(8,128)(2,1)S(1)} %convert_element_type.32), kind=kOutput, calls=%fused_computation.4 | convolution fusion | flops 2147483648 | bytes 23068672 | tf_op jit(solution)/shard_map/hvi,hvg->hig/dot_general | solution.py:63
  407.0 10.0 %fusion.70 = bf16[1,8,1024,128]{2,3,1,0:T(8,128)(2,1)S(1)} fusion(f32[8,128,1024]{2,1,0:T(8,128)} %fusion.4, bf16[2,8,1024,1024]{3,2,1,0:T(8,128)(2,1)} %param.3, bf16[2,8,1024,128]{2,3,1,0:T(8,128)(2,1)} %copy-done.2), kind=kOutput, calls=%fused_computation.157 | convolution fusion | flops 2149580800 | bytes 25165824 | tf_op jit(solution)/shard_map/hvi,hvg->hig/dot_general | solution.py:61
  441.6 111.7 %all_to_all.41 = bf16[16,2,8,64,128]{4,3,2,1,0:T(8,128)(2,1)S(1)} all-to-all(bf16[16,2,8,64,128]{4,3,2,1,0:T(8,128)(2,1)} %copy.95), channel_id=1, replica_groups=mesh['grp'=2,'freq'=16] {'freq'}, dimensions={0} | all-to-all | bytes 8388608 | tf_op jit(solution)/shard_map/all_to_all | solution.py:14
  558.8 11.4 %multiply_reduce_fusion = (f32[]{:T(128)}, f32[]{:T(128)}, f32[256,8192]{1,0:T(8,128)}) fusion(s32[8192]{0:T(1024)S(1)} %bitcast.315, f32[]{:T(128)S(6)} %mul.210, f32[256,8192]{1,0:T(8,128)S(1)} %bitcast.294, f32[256,8192]{1,0:T(8,128)S(1)} %fusion.73, bf16[16,8,64,128]{3,2,1,0:T(8,128)(2,1)S(1)} %get-tuple-element.18), kind=kOutput, calls=%fused_computation.113 | convolution fusion | flops 3240591360 | bytes 27295756 | tf_op jit(solution)/shard_map/dot_general | solution.py:47
  570.1 34.3 %all-reduce = (f32[]{:T(128)}, f32[]{:T(128)}, f32[]{:T(128)}) all-reduce(f32[]{:T(128)} %get-tuple-element.12, f32[]{:T(128)} %get-tuple-element.6, f32[]{:T(128)} %get-tuple-element.5), channel_id=1, replica_groups=mesh['grp'=2,'freq'=16] {'freq'}, use_global_device_ids=true, to_apply=%region_5.6 | all-reduce | flops 3 | bytes 24 | tf_op jit(solution)/shard_map/psum | solution.py:31
  642.3 68.6 %all-to-all-done.3 = bf16[2,128,64,128]{3,2,0,1:T(8,128)(2,1)} async-done(((bf16[2,128,64,128]{3,2,0,1:T(8,128)(2,1)}), bf16[2,128,64,128]{3,2,0,1:T(8,128)(2,1)}, u32[]{:S(2)}, u32[]{:S(2)}) %all-to-all-start.3) | async-done | bytes 4194336 | tf_op jit(solution)/shard_map/all_to_all | solution.py:89
  716.5 14.0 %fusion.2 = f32[8,128,1024]{2,1,0:T(8,128)} fusion(bf16[8,1024,128]{2,1,0:T(8,128)(2,1)} %bitcast.306, bf16[2,8,1024,1024]{3,2,1,0:T(8,128)(2,1)} %param.3), kind=kOutput, calls=%fused_computation.2 | convolution fusion | flops 2147483648 | bytes 23068672 | tf_op jit(solution)/shard_map/ptx,pxi->pti/dot_general | solution.py:96
  732.1 14.2 %fusion = f32[8,128,1024]{2,1,0:T(8,128)} fusion(bf16[8,1024,128]{2,1,0:T(8,128)(2,1)} %bitcast.310, bf16[2,8,1024,1024]{3,2,1,0:T(8,128)(2,1)} %param.3), kind=kOutput, calls=%fused_computation | convolution fusion | flops 2147483648 | bytes 23068672 | tf_op jit(solution)/shard_map/ptx,pxi->pti/dot_general | solution.py:101
  746.4 10.7 %subtract_bitcast_fusion = f32[1,8,1024,128]{2,3,1,0:T(8,128)S(1)} fusion(f32[8,128,1024]{2,1,0:T(8,128)} %fusion.2, bf16[8,1024,128]{2,1,0:T(8,128)(2,1)} %bitcast.311, bf16[2,8,1024,1024]{3,2,1,0:T(8,128)(2,1)} %param.3), kind=kOutput, calls=%fused_computation.127 | convolution fusion | flops 2148532224 | bytes 27262976 | tf_op jit(solution)/shard_map/ptx,pxi->pti/dot_general | solution.py:94
  757.1 11.2 %add_bitcast_fusion = f32[1,8,1024,128]{2,3,1,0:T(8,128)} fusion(f32[8,128,1024]{2,1,0:T(8,128)} %fusion, bf16[8,1024,128]{2,1,0:T(8,128)(2,1)S(1)} %bitcast.307, bf16[2,8,1024,1024]{3,2,1,0:T(8,128)(2,1)} %param.3), kind=kOutput, calls=%fused_computation.126 | convolution fusion | flops 2148532224 | bytes 27262976 | tf_op jit(solution)/shard_map/ptx,pxi->pti/dot_general | solution.py:99
  782.8 48.3 %psum.47 = f32[]{:T(128)} all-reduce(f32[]{:T(128)} %fusion.40), channel_id=1, replica_groups=mesh['grp'=2,'freq'=16] {'freq'}, use_global_device_ids=true, to_apply=%region_11.12 | all-reduce | flops 1 | bytes 8 | tf_op jit(solution)/shard_map/psum | solution.py:31
  (89 shorter events, 173.8 us)
Async XLA Ops:
  151.4 4.4 copy-start.5
  203.4 10.7 %copy-start = (f32[256,8192]{1,0:T(8,128)S(1)}, f32[256,8192]{1,0:T(8,128)}, u32[]{:S(2)}) copy-start(f32[256,8192]{1,0:T(8,128)} %get-tuple-element.25) | copy-start | bytes 25165828
  225.9 82.0 %all-to-all-start.1 = ((bf16[2,128,64,128]{3,2,0,1:T(8,128)(2,1)}), bf16[2,128,64,128]{3,2,0,1:T(8,128)(2,1)}, u32[]{:S(2)}, u32[]{:S(2)}) async-start(bf16[2,128,64,128]{3,2,0,1:T(8,128)(2,1)} %pad_maximum_fusion), calls=%async_computation.1 | async-start | bytes 8388608 | tf_op jit(solution)/shard_map/all_to_all | solution.py:89
  343.2 11.1 %copy-start.3 = (bf16[1,8,16,64,128]{4,3,2,1,0:T(8,128)(2,1)S(1)}, bf16[1,8,16,64,128]{4,3,2,1,0:T(8,128)(2,1)}, u32[]{:S(2)}) copy-start(bf16[1,8,16,64,128]{4,3,2,1,0:T(8,128)(2,1)} %copy.83) | copy-start | bytes 6291460
  371.9 3.2 copy-start.1
  375.8 21.7 %copy-start.2 = (bf16[2,8,1024,128]{2,3,1,0:T(8,128)(2,1)}, bf16[2,8,1024,128]{2,3,1,0:T(8,128)(2,1)S(1)}, u32[]{:S(2)}) copy-start(bf16[2,8,1024,128]{2,3,1,0:T(8,128)(2,1)S(1)} %convert_element_type.32) | copy-start | bytes 12582916
  553.3 5.4 slice-start
  554.4 4.3 slice-start.1
  554.4 4.3 copy-start.6
  628.8 82.0 %all-to-all-start.3 = ((bf16[2,128,64,128]{3,2,0,1:T(8,128)(2,1)}), bf16[2,128,64,128]{3,2,0,1:T(8,128)(2,1)}, u32[]{:S(2)}, u32[]{:S(2)}) async-start(bf16[2,128,64,128]{3,2,0,1:T(8,128)(2,1)} %pad_maximum_fusion.1), calls=%async_computation.3 | async-start | bytes 8388608 | tf_op jit(solution)/shard_map/all_to_all | solution.py:89
  746.4 10.7 %copy-start.4 = (bf16[1,8,16,64,128]{4,3,2,1,0:T(8,128)(2,1)S(1)}, bf16[1,8,16,64,128]{4,3,2,1,0:T(8,128)(2,1)}, u32[]{:S(2)}) copy-start(bf16[1,8,16,64,128]{4,3,2,1,0:T(8,128)(2,1)} %copy.102) | copy-start | bytes 6291460
